TPU v7x, 32 devices: a whole 2x2x4 slice. The times are simulated.
32 devices in a mesh: rep: 8 (over z, core), tp: 4 (over y, x).
Axes of the slice: x: 2, y: 2, z: 4, core: 2. Of those that a mesh axis runs over, the one named last changes fastest.
Arguments:
- delta_query: bfloat16 [8, 2, 2048, 3072], P('rep', None, None, 'tp'), may hold values from -6 to 6
- master_query: float32 [2, 2048, 3072], P(None, 'rep', 'tp'), may hold values from -3 to 3
- moment_query: float32 [2, 2048, 3072], P(None, 'rep', 'tp'), may hold values from -3 to 3
- delta_latent: bfloat16 [8, 2, 512, 4096], P('rep', None, None, 'tp'), may hold values from -6 to 6
- master_latent: float32 [2, 512, 4096], P(None, 'rep', 'tp'), may hold values from -3 to 3
- moment_latent: float32 [2, 512, 4096], P(None, 'rep', 'tp'), may hold values from -3 to 3
- delta_output: bfloat16 [8, 2, 2048, 2048], P('rep', None, 'tp'), may hold values from -6 to 6
- master_output: float32 [2, 2048, 2048], P(None, 'tp', 'rep'), may hold values from -3 to 3
- moment_output: float32 [2, 2048, 2048], P(None, 'tp', 'rep'), may hold values from -3 to 3
Outputs:
- params_query: bfloat16 [2, 2048, 3072], P(None, None, 'tp')
- new_master_query: float32 [2, 2048, 3072], P(None, 'rep', 'tp')
- new_moment_query: float32 [2, 2048, 3072], P(None, 'rep', 'tp')
- params_latent: bfloat16 [2, 512, 4096], P(None, None, 'tp')
- new_master_latent: float32 [2, 512, 4096], P(None, 'rep', 'tp')
- new_moment_latent: float32 [2, 512, 4096], P(None, 'rep', 'tp')
- params_output: bfloat16 [2, 2048, 2048], P(None, 'tp')
- new_master_output: float32 [2, 2048, 2048], P(None, 'tp', 'rep')
- new_moment_output: float32 [2, 2048, 2048], P(None, 'tp', 'rep')
All inputs are finite; a program needn't handle non-finite values.
Results may differ from a plain program's by a relative error of at most 0.012.
Values may be sent and summed in bfloat16 or wider, within the bound.
A program may use at most 128 MiB of HBM per device.

v0:
```python
import jax
import jax.numpy as jnp
from jax import lax
from jax.sharding import PartitionSpec as P

OUTER_RATE = 0.7
OUTER_MOMENTUM = 0.9


def nesterov(totals, master, moment, replica_count):
    average = totals / replica_count
    momentum = OUTER_MOMENTUM * moment + average
    updated = master - OUTER_RATE * (average + OUTER_MOMENTUM * momentum)
    return (updated, momentum)


def outer_step(
    delta_query,
    master_query,
    moment_query,
    delta_latent,
    master_latent,
    moment_latent,
    delta_output,
    master_output,
    moment_output,
):
    replica_count = lax.axis_size("rep")
    query_totals = lax.psum_scatter(
        delta_query[0].astype(jnp.float32).astype(jnp.bfloat16),
        "rep",
        scatter_dimension=1,
        tiled=True,
    ).astype(jnp.float32)
    latent_totals = lax.psum_scatter(
        delta_latent[0].astype(jnp.float32).astype(jnp.bfloat16),
        "rep",
        scatter_dimension=1,
        tiled=True,
    ).astype(jnp.float32)
    output_totals = lax.psum_scatter(
        delta_output[0].astype(jnp.float32).astype(jnp.bfloat16),
        "rep",
        scatter_dimension=2,
        tiled=True,
    ).astype(jnp.float32)
    query_master, query_moment = nesterov(query_totals, master_query, moment_query, replica_count)
    latent_master, latent_moment = nesterov(
        latent_totals, master_latent, moment_latent, replica_count
    )
    output_master, output_moment = nesterov(
        output_totals, master_output, moment_output, replica_count
    )
    query_params = lax.all_gather(query_master.astype(jnp.bfloat16), "rep", axis=1, tiled=True)
    latent_params = lax.all_gather(latent_master.astype(jnp.bfloat16), "rep", axis=1, tiled=True)
    output_params = lax.all_gather(output_master.astype(jnp.bfloat16), "rep", axis=2, tiled=True)
    return (
        query_params,
        query_master,
        query_moment,
        latent_params,
        latent_master,
        latent_moment,
        output_params,
        output_master,
        output_moment,
    )


def on_device(
    delta_query,
    master_query,
    moment_query,
    delta_latent,
    master_latent,
    moment_latent,
    delta_output,
    master_output,
    moment_output,
):
    return outer_step(
        delta_query,
        master_query,
        moment_query,
        delta_latent,
        master_latent,
        moment_latent,
        delta_output,
        master_output,
        moment_output,
    )


def solution(mesh):
    placed = (
        P("rep", None, None, "tp"),
        P(None, "rep", "tp"),
        P(None, "rep", "tp"),
        P("rep", None, None, "tp"),
        P(None, "rep", "tp"),
        P(None, "rep", "tp"),
        P("rep", None, "tp", None),
        P(None, "tp", "rep"),
        P(None, "tp", "rep"),
    )
    return jax.shard_map(
        on_device,
        mesh=mesh,
        in_specs=placed,
        out_specs=(
            P(None, None, "tp"),
            P(None, "rep", "tp"),
            P(None, "rep", "tp"),
            P(None, None, "tp"),
            P(None, "rep", "tp"),
            P(None, "rep", "tp"),
            P(None, "tp", None),
            P(None, "tp", "rep"),
            P(None, "tp", "rep"),
        ),
        check_vma=False,
    )
```

profile of v0, /device:TPU:0, one launch (start us, length us, event | category | flops | bytes accessed | tf_op | source)
XLA Modules:
  0.0 332.2 jit_solution(7297838098868273898)
XLA Ops:
  7.2 0.0 reduce-scatter.6.cloned.1.call-start
  7.2 0.7 reduce-scatter.6.cloned.1.call-update
  7.9 0.0 reduce-scatter.8.cloned.1.call-start
  8.0 0.7 reduce-scatter.8.cloned.1.call-update
  8.7 0.0 reduce-scatter.4.cloned.1.call-start
  8.7 0.0 copy-start.4
  8.7 0.0 copy-start.5
  8.7 0.7 reduce-scatter.4.cloned.1.call-update
  9.4 0.0 all-gather.6.cloned.1.call-start
  9.4 39.6 %reduce-scatter.6.cloned.1.call-done = bf16[2,64,1024]{2,1,0:T(8,128)(2,1)} async-done(((bf16[2,512,1024]{2,1,0:T(8,128)(2,1)}), bf16[2,64,1024]{2,1,0:T(8,128)(2,1)}) %reduce-scatter.6.cloned.1.call-update) | async-done | bytes 262160 | tf_op jit(solution)/shard_map/reduce_scatter | solution.py:35
  49.1 0.0 copy-done.4
  49.1 0.0 copy-done.5
  49.1 2.1 fusion.1
  51.2 0.0 all-gather.6.cloned.1.call-update
  51.2 0.0 all-gather.8.cloned.1.call-start
  51.3 48.6 %reduce-scatter.8.cloned.1.call-done = bf16[2,512,256]{2,1,0:T(8,128)(2,1)} async-done(((bf16[2,512,2048]{2,1,0:T(8,128)(2,1)}), bf16[2,512,256]{2,1,0:T(8,128)(2,1)}) %reduce-scatter.8.cloned.1.call-update) | async-done | bytes 524304 | tf_op jit(solution)/shard_map/reduce_scatter | solution.py:41
  99.9 3.6 %fusion = (bf16[2,512,256]{2,1,0:T(8,128)(2,1)}, f32[2,512,256]{2,1,0:T(8,128)}, f32[2,512,256]{2,1,0:T(8,128)}) fusion(f32[2,512,256]{2,1,0:T(8,128)} %param.16, bf16[2,512,256]{2,1,0:T(8,128)(2,1)} %reduce-scatter.8.cloned.1.call-done, f32[2,512,256]{2,1,0:T(8,128)} %param.17), kind=kLoop, calls=%fused_computation.9 | loop fusion | flops 2359296 | bytes 5242880 | tf_op jit(solution)/shard_map/convert_element_type | solution.py:56
  103.5 0.0 all-gather.8.cloned.1.call-update
  103.6 0.0 all-gather.4.cloned.1.call-start
  103.6 66.8 %reduce-scatter.4.cloned.1.call-done = bf16[2,256,768]{2,1,0:T(8,128)(2,1)} async-done(((bf16[2,2048,768]{2,1,0:T(8,128)(2,1)}), bf16[2,256,768]{2,1,0:T(8,128)(2,1)}) %reduce-scatter.4.cloned.1.call-update) | async-done | bytes 786448 | tf_op jit(solution)/shard_map/reduce_scatter | solution.py:29
  170.4 0.0 copy-done.2
  170.4 0.0 copy-done.3
  170.4 3.5 %fusion.2 = (bf16[2,256,768]{2,1,0:T(8,128)(2,1)}, f32[2,256,768]{2,1,0:T(8,128)}, f32[2,256,768]{2,1,0:T(8,128)}) fusion(f32[2,256,768]{2,1,0:T(8,128)S(1)} %copy-done.2, bf16[2,256,768]{2,1,0:T(8,128)(2,1)} %reduce-scatter.4.cloned.1.call-done, f32[2,256,768]{2,1,0:T(8,128)S(1)} %copy-done.3), kind=kLoop, calls=%fused_computation.11 | loop fusion | flops 3538944 | bytes 7864320 | tf_op jit(solution)/shard_map/convert_element_type | solution.py:54
  173.9 0.0 all-gather.4.cloned.1.call-update
  174.0 26.2 %all-gather.6.cloned.1.call-done = bf16[2,512,1024]{2,1,0:T(8,128)(2,1)} async-done(((bf16[2,64,1024]{2,1,0:T(8,128)(2,1)}), bf16[2,512,1024]{2,1,0:T(8,128)(2,1)}) %all-gather.6.cloned.1.call-update) | async-done | bytes 2097168 | tf_op jit(solution)/shard_map/all_gather | solution.py:55
  200.1 49.3 %all-gather.8.cloned.1.call-done = bf16[2,512,2048]{2,1,0:T(8,128)(2,1)} async-done(((bf16[2,512,256]{2,1,0:T(8,128)(2,1)}), bf16[2,512,2048]{2,1,0:T(8,128)(2,1)}) %all-gather.8.cloned.1.call-update) | async-done | bytes 4194320 | tf_op jit(solution)/shard_map/all_gather | solution.py:56
  249.4 64.9 %all-gather.4.cloned.1.call-done = bf16[2,2048,768]{2,1,0:T(8,128)(2,1)} async-done(((bf16[2,256,768]{2,1,0:T(8,128)(2,1)}), bf16[2,2048,768]{2,1,0:T(8,128)(2,1)}) %all-gather.4.cloned.1.call-update) | async-done | bytes 6291472 | tf_op jit(solution)/shard_map/all_gather | solution.py:54
  314.3 6.0 %copy.21 = bf16[2,2048,768]{2,1,0:T(8,128)(2,1)} copy(bf16[2,2048,768]{2,1,0:T(8,128)(2,1)} %all-gather.4.cloned.1.call-done) | data formatting | bytes 12582912
  320.4 0.0 copy-done.1
  320.4 1.3 copy.22
  321.7 1.6 copy-done
  323.3 2.0 copy.23
  (4 shorter events, 0.0 us)
Async XLA Ops:
  7.2 41.9 %reduce-scatter.6.cloned.1.call-start = ((), (), s32[]{:S(2)}) async-start(), calls=%async_computation.5 | async-start | bytes 2359296 | tf_op jit(solution)/shard_map/reduce_scatter | solution.py:35
  7.9 92.0 %reduce-scatter.8.cloned.1.call-start = ((), (), s32[]{:S(2)}) async-start(), calls=%async_computation.7 | async-start | bytes 4718592 | tf_op jit(solution)/shard_map/reduce_scatter | solution.py:41
  8.7 161.8 %reduce-scatter.4.cloned.1.call-start = ((), (), s32[]{:S(2)}) async-start(), calls=%async_computation.3 | async-start | bytes 7077888 | tf_op jit(solution)/shard_map/reduce_scatter | solution.py:29
  8.7 40.4 %copy-start.4 = (f32[2,64,1024]{2,1,0:T(8,128)S(1)}, f32[2,64,1024]{2,1,0:T(8,128)}, u32[]{:S(2)}) copy-start(f32[2,64,1024]{2,1,0:T(8,128)} %param.13) | copy-start | bytes 1572868
  8.7 40.3 %copy-start.5 = (f32[2,64,1024]{2,1,0:T(8,128)S(1)}, f32[2,64,1024]{2,1,0:T(8,128)}, u32[]{:S(2)}) copy-start(f32[2,64,1024]{2,1,0:T(8,128)} %param.14) | copy-start | bytes 1572868
  9.4 190.7 %all-gather.6.cloned.1.call-start = ((), (), s32[]{:S(2)}) async-start(), calls=%async_computation.6 | async-start | bytes 2359296 | tf_op jit(solution)/shard_map/all_gather | solution.py:55
  51.2 198.2 %all-gather.8.cloned.1.call-start = ((), (), s32[]{:S(2)}) async-start(), calls=%async_computation.8 | async-start | bytes 4718592 | tf_op jit(solution)/shard_map/all_gather | solution.py:56
  99.9 70.5 %copy-start.2 = (f32[2,256,768]{2,1,0:T(8,128)S(1)}, f32[2,256,768]{2,1,0:T(8,128)}, u32[]{:S(2)}) copy-start(f32[2,256,768]{2,1,0:T(8,128)} %param.10) | copy-start | bytes 4718596
  99.9 70.5 %copy-start.3 = (f32[2,256,768]{2,1,0:T(8,128)S(1)}, f32[2,256,768]{2,1,0:T(8,128)}, u32[]{:S(2)}) copy-start(f32[2,256,768]{2,1,0:T(8,128)} %param.11) | copy-start | bytes 4718596
  103.6 210.8 %all-gather.4.cloned.1.call-start = ((), (), s32[]{:S(2)}) async-start(), calls=%async_computation.4 | async-start | bytes 7077888 | tf_op jit(solution)/shard_map/all_gather | solution.py:54
  314.3 6.0 %copy-start.1 = (bf16[2,512,1024]{2,1,0:T(8,128)(2,1)S(1)}, bf16[2,512,1024]{2,1,0:T(8,128)(2,1)}, u32[]{:S(2)}) copy-start(bf16[2,512,1024]{2,1,0:T(8,128)(2,1)} %all-gather.6.cloned.1.call-done) | copy-start | bytes 6291460
  320.4 2.9 copy-start
Sparse Core Ops, SparseCore 0:
  10.3 38.7 reduce-scatter.5
  51.3 48.5 reduce-scatter.7
  102.2 68.1 reduce-scatter.3
  172.5 27.6 all-gather.5
  202.1 47.1 all-gather.7
  251.4 62.8 all-gather.3
where the time goes:
time: 332 us
  waiting for transfers between devices  298 us (90%)
  between operations  14.1 us (4%)
  local copies, waits for them, and re-layouts  11 us (3%)
  other arithmetic  9.27 us (3%)
    reduce_scatter x1, waiting for transfers between devices, outer_step(): lax.psum_scatter(delta_query[0].astype(jnp.float32).astype(jnp.bfloat16),...  66.8 us
    all_gather x1, waiting for transfers between devices, outer_step(): lax.all_gather(query_master.astype(jnp.bfloat16), 'rep', axis=1, tiled=True)  64.9 us
    all_gather x1, waiting for transfers between devices, outer_step(): lax.all_gather(output_master.astype(jnp.bfloat16), 'rep', axis=2, tiled=T...  49.3 us
    reduce_scatter x1, waiting for transfers between devices, outer_step(): lax.psum_scatter(delta_output[0].astype(jnp.float32).astype(jnp.bfloat16)...  48.6 us
    reduce_scatter x1, waiting for transfers between devices, outer_step(): lax.psum_scatter(delta_latent[0].astype(jnp.float32).astype(jnp.bfloat16)...  39.6 us
    all_gather x1, waiting for transfers between devices, outer_step(): lax.all_gather(latent_master.astype(jnp.bfloat16), 'rep', axis=1, tiled=T...  26.2 us
    unnamed x15, local copies, waits for them, and re-layouts  11 us
  transfers between devices with their start and end apart: 6, of which 6 were waited for; matrix products, arithmetic and copies ran while one was open for 3% of the time, Pallas kernels for 0%

commit v1 on v0

--- a/solution.py
+++ b/solution.py
@@ -51,7 +51,12 @@
     output_master, output_moment = nesterov(
         output_totals, master_output, moment_output, replica_count
     )
-    query_params = lax.all_gather(query_master.astype(jnp.bfloat16), "rep", axis=1, tiled=True)
+    query_params = jnp.concatenate(
+        lax.all_to_all(
+            jnp.stack([query_master.astype(jnp.bfloat16)] * lax.axis_size("rep")), "rep", 0, 0
+        ),
+        axis=1,
+    )
     latent_params = lax.all_gather(latent_master.astype(jnp.bfloat16), "rep", axis=1, tiled=True)
     output_params = lax.all_gather(output_master.astype(jnp.bfloat16), "rep", axis=2, tiled=True)
     return (

time: 332 us -> 379 us (1.14)
  waiting for transfers between devices: 298 us -> 337 us
  starting transfers between devices: 0.24 us -> 5.08 us
    all_gather x1 -> x0, waiting for transfers between devices: 64.9 us -> none  [outer_step(): lax.all_gather(query_master.astype(jnp.bfloat16), 'rep', axis=1, tiled=True)]
    all_gather x1, waiting for transfers between devices: 26.2 us -> 82.3 us  [outer_step(): lax.all_gather(latent_master.astype(jnp.bfloat16), 'rep', axis=1, tiled=T...]
    reduce_scatter x1, waiting for transfers between devices: 48.6 us -> 95.7 us  [outer_step(): lax.psum_scatter(delta_output[0].astype(jnp.float32).astype(jnp.bfloat16)...]
    all_to_all x0 -> x1, local copies, waits for them, and re-layouts: none -> 6.04 us  [outer_step(): lax.all_to_all(jnp.stack([query_master.astype(jnp.bfloat16)] * lax.axis_s...]
    unnamed x15 -> x14, local copies, waits for them, and re-layouts: 11 us -> 4.98 us
    all_to_all x0 -> x1, starting transfers between devices: none -> 4.89 us  [outer_step(): lax.all_to_all(jnp.stack([query_master.astype(jnp.bfloat16)] * lax.axis_s...]
  transfers between devices with their start and end apart: 6 -> 6, of which waited for: 6 -> 5; matrix products, arithmetic and copies ran while one was open for 3% -> 3% of each run, Pallas kernels for 0% -> 0%
where the time goes in v1:
time: 379 us; the launch traced here: 378 us
  waiting for transfers between devices  337 us (89%)
  local copies, waits for them, and re-layouts  14.3 us (4%)
  between operations  13.8 us (4%)
  other arithmetic  8.58 us (2%)
  starting transfers between devices  5.08 us (1%)
    reduce_scatter x1, waiting for transfers between devices, outer_step(): lax.psum_scatter(delta_output[0].astype(jnp.float32).astype(jnp.bfloat16)...  95.7 us
    all_gather x1, waiting for transfers between devices, outer_step(): lax.all_gather(latent_master.astype(jnp.bfloat16), 'rep', axis=1, tiled=T...  82.3 us
    reduce_scatter x1, waiting for transfers between devices, outer_step(): lax.psum_scatter(delta_query[0].astype(jnp.float32).astype(jnp.bfloat16),...  68.1 us
    all_gather x1, waiting for transfers between devices, outer_step(): lax.all_gather(output_master.astype(jnp.bfloat16), 'rep', axis=2, tiled=T...  48.7 us
    reduce_scatter x1, waiting for transfers between devices, outer_step(): lax.psum_scatter(delta_latent[0].astype(jnp.float32).astype(jnp.bfloat16)...  39.6 us
  transfers between devices with their start and end apart: 6, of which 5 were waited for; matrix products, arithmetic and copies ran while one was open for 3% of the time, Pallas kernels for 0%

profile of v1, /device:TPU:0, one launch (start us, length us, event | category | flops | bytes accessed | tf_op | source)
XLA Modules:
  0.0 378.4 jit_solution(7937190650873301014)
XLA Ops:
  7.2 0.0 reduce-scatter.6.cloned.1.call-start
  7.2 0.7 reduce-scatter.6.cloned.1.call-update
  7.9 0.0 reduce-scatter.4.cloned.1.call-start
  8.0 0.7 reduce-scatter.4.cloned.1.call-update
  8.7 0.0 reduce-scatter.8.cloned.1.call-start
  8.7 0.0 copy-start.3
  8.7 0.7 reduce-scatter.8.cloned.1.call-update
  9.4 0.0 copy-start.2
  9.4 0.0 all-gather.3.cloned.1.call-start
  9.5 39.6 %reduce-scatter.6.cloned.1.call-done = bf16[2,64,1024]{2,1,0:T(8,128)(2,1)} async-done(((bf16[2,512,1024]{2,1,0:T(8,128)(2,1)}), bf16[2,64,1024]{2,1,0:T(8,128)(2,1)}) %reduce-scatter.6.cloned.1.call-update) | async-done | bytes 262160 | tf_op jit(solution)/shard_map/reduce_scatter | solution.py:35
  49.1 2.5 fusion.1
  51.6 0.0 all-gather.3.cloned.1.call-update
  51.6 68.1 %reduce-scatter.4.cloned.1.call-done = bf16[2,256,768]{2,1,0:T(8,128)(2,1)} async-done(((bf16[2,2048,768]{2,1,0:T(8,128)(2,1)}), bf16[2,256,768]{2,1,0:T(8,128)(2,1)}) %reduce-scatter.4.cloned.1.call-update) | async-done | bytes 786448 | tf_op jit(solution)/shard_map/reduce_scatter | solution.py:29
  119.7 0.0 copy-done.3
  119.7 0.0 copy-done.2
  119.7 3.2 fusion.2
  123.0 3.3 stack.2
  126.3 4.9 %all-to-all-start = ((bf16[8,2,256,768]{3,2,1,0:T(8,128)(2,1)}), bf16[8,2,256,768]{3,2,1,0:T(8,128)(2,1)}, u32[]{:S(2)}, u32[]{:S(2)}) async-start(bf16[8,2,256,768]{3,2,1,0:T(8,128)(2,1)} %stack.2), calls=%async_computation.1 | async-start | bytes 12582912 | tf_op jit(solution)/shard_map/all_to_all | solution.py:55
  131.2 0.0 all-gather.5.cloned.1.call-start
  131.2 95.7 %reduce-scatter.8.cloned.1.call-done = bf16[2,512,256]{2,1,0:T(8,128)(2,1)} async-done(((bf16[2,512,2048]{2,1,0:T(8,128)(2,1)}), bf16[2,512,256]{2,1,0:T(8,128)(2,1)}) %reduce-scatter.8.cloned.1.call-update) | async-done | bytes 524304 | tf_op jit(solution)/shard_map/reduce_scatter | solution.py:41
  227.0 0.0 copy-done.4
  227.0 0.0 copy-done.5
  227.0 2.8 fusion
  229.8 0.0 all-gather.5.cloned.1.call-update
  229.8 82.3 %all-gather.3.cloned.1.call-done = bf16[2,512,1024]{2,1,0:T(8,128)(2,1)} async-done(((bf16[2,64,1024]{2,1,0:T(8,128)(2,1)}), bf16[2,512,1024]{2,1,0:T(8,128)(2,1)}) %all-gather.3.cloned.1.call-update) | async-done | bytes 2097168 | tf_op jit(solution)/shard_map/all_gather | solution.py:60
  312.1 48.7 %all-gather.5.cloned.1.call-done = bf16[2,512,2048]{2,1,0:T(8,128)(2,1)} async-done(((bf16[2,512,256]{2,1,0:T(8,128)(2,1)}), bf16[2,512,2048]{2,1,0:T(8,128)(2,1)}) %all-gather.5.cloned.1.call-update) | async-done | bytes 4194320 | tf_op jit(solution)/shard_map/all_gather | solution.py:61
  360.8 0.0 all-to-all-done
  360.8 6.0 %copy.18 = bf16[8,2,256,768]{3,2,0,1:T(8,128)(2,1)} copy(bf16[8,2,256,768]{3,2,1,0:T(8,128)(2,1)} %all-to-all-done) | data formatting | bytes 12582912 | tf_op jit(solution)/shard_map/all_to_all | solution.py:55
  366.9 0.0 copy-done.1
  366.9 1.3 copy.21
  368.2 1.6 copy-done
  369.8 2.0 copy.22
  (4 shorter events, 0.0 us)
Async XLA Ops:
  7.2 41.9 %reduce-scatter.6.cloned.1.call-start = ((), (), s32[]{:S(2)}) async-start(), calls=%async_computation.5 | async-start | bytes 2359296 | tf_op jit(solution)/shard_map/reduce_scatter | solution.py:35
  7.9 111.8 %reduce-scatter.4.cloned.1.call-start = ((), (), s32[]{:S(2)}) async-start(), calls=%async_computation.4 | async-start | bytes 7077888 | tf_op jit(solution)/shard_map/reduce_scatter | solution.py:29
  8.7 218.3 %reduce-scatter.8.cloned.1.call-start = ((), (), s32[]{:S(2)}) async-start(), calls=%async_computation.7 | async-start | bytes 4718592 | tf_op jit(solution)/shard_map/reduce_scatter | solution.py:41
  8.7 111.0 %copy-start.3 = (f32[2,256,768]{2,1,0:T(8,128)S(1)}, f32[2,256,768]{2,1,0:T(8,128)}, u32[]{:S(2)}) copy-start(f32[2,256,768]{2,1,0:T(8,128)} %param.11) | copy-start | bytes 4718596
  9.4 110.3 %copy-start.2 = (f32[2,256,768]{2,1,0:T(8,128)S(1)}, f32[2,256,768]{2,1,0:T(8,128)}, u32[]{:S(2)}) copy-start(f32[2,256,768]{2,1,0:T(8,128)} %param.10) | copy-start | bytes 4718596
  9.4 302.7 %all-gather.3.cloned.1.call-start = ((), (), s32[]{:S(2)}) async-start(), calls=%async_computation.6 | async-start | bytes 2359296 | tf_op jit(solution)/shard_map/all_gather | solution.py:60
  126.3 100.7 %copy-start.4 = (f32[2,512,256]{2,1,0:T(8,128)S(1)}, f32[2,512,256]{2,1,0:T(8,128)}, u32[]{:S(2)}) copy-start(f32[2,512,256]{2,1,0:T(8,128)} %param.16) | copy-start | bytes 3145732
  126.3 100.7 %copy-start.5 = (f32[2,512,256]{2,1,0:T(8,128)S(1)}, f32[2,512,256]{2,1,0:T(8,128)}, u32[]{:S(2)}) copy-start(f32[2,512,256]{2,1,0:T(8,128)} %param.17) | copy-start | bytes 3145732
  126.3 234.5 %all-to-all-start = ((bf16[8,2,256,768]{3,2,1,0:T(8,128)(2,1)}), bf16[8,2,256,768]{3,2,1,0:T(8,128)(2,1)}, u32[]{:S(2)}, u32[]{:S(2)}) async-start(bf16[8,2,256,768]{3,2,1,0:T(8,128)(2,1)} %stack.2), calls=%async_computation.1 | async-start | bytes 12582912 | tf_op jit(solution)/shard_map/all_to_all | solution.py:55
  131.2 229.6 %all-gather.5.cloned.1.call-start = ((), (), s32[]{:S(2)}) async-start(), calls=%async_computation.8 | async-start | bytes 4718592 | tf_op jit(solution)/shard_map/all_gather | solution.py:61
  312.1 54.8 %copy-start.1 = (bf16[2,512,1024]{2,1,0:T(8,128)(2,1)S(1)}, bf16[2,512,1024]{2,1,0:T(8,128)(2,1)}, u32[]{:S(2)}) copy-start(bf16[2,512,1024]{2,1,0:T(8,128)(2,1)} %all-gather.3.cloned.1.call-done) | copy-start | bytes 6291460
  366.9 2.9 copy-start
Sparse Core Ops, SparseCore 0:
  10.3 38.7 reduce-scatter.5
  51.4 68.3 reduce-scatter.3
  122.0 104.9 reduce-scatter.7
  229.0 83.0 all-gather.2
  314.1 46.6 all-gather.4
